TPU v7x, 32 devices: a whole 2x2x4 slice. The times are simulated.
32 devices in a mesh: gx: 8 (over y, x, core), gy: 4 (over z).
Axes of the slice: x: 2, y: 2, z: 4, core: 2. Of those that a mesh axis runs over, the one named last changes fastest.
Arguments:
- node_disp: float32 [2, 256, 1024], P(None, 'gx', 'gy'), may hold values from -0.24 to 0.24
- node_vel: float32 [2, 256, 1024], P(None, 'gx', 'gy'), may hold values from -6 to 6
- node_mass: float32 [256, 1024], P('gx', 'gy'), may hold values from 0.5 to 2
- zone_mass: float32 [256, 1024], P('gx', 'gy'), may hold values from 0.5 to 2
- zone_energy: float32 [256, 1024], P('gx', 'gy'), may hold values from 0.3 to 7.5
- master_block: bfloat16 [32, 4, 1024], P(('gx', 'gy')), may hold values from -3 to 3, as said below
- owner: int32 [1], replicated, may hold values from 0 to 31
- pair_node: int32 [32, 1024], P(('gx', 'gy')), may hold values from 0 to 8191
- pair_segment: int32 [32, 1024], P(('gx', 'gy')), may hold values from 0 to 1022
- pair_side: int32 [32, 1024], P(('gx', 'gy')), may hold values 0 or 1
- pair_count: int32 [32], P(('gx', 'gy')), may hold values from 0 to 1024, as said below
Outputs:
- new_vel: float32 [2, 256, 1024], P(None, 'gx', 'gy')
- new_disp: float32 [2, 256, 1024], P(None, 'gx', 'gy')
- master_impulse: float32 [3, 1024], P(None, ('gx', 'gy'))
Inputs may be any that keep to these rules, and one draw needn't show every extreme that they name: `pair_node`: local node numbers, row-major over a device's 32 x 256 block. `pair_count`: at most 1024; one device has exactly 1024 in every draw; slots at or past a device's count are not pairs. `master_block`: rows 0 and 1 lie within -0.25 to 0.25.
All inputs are finite; a program needn't handle non-finite values. No bound on the sum of `pair_side` on one device may be relied on, other than what follows from the above.
Results may differ from a plain program's by a relative error of at most 0.0015.
Values may be sent and summed in bfloat16 or wider, within the bound.
A program may use at most 128 MiB of HBM per device.

v0:
```python
import jax
import jax.numpy as jnp
from jax import lax
from jax.sharding import PartitionSpec as P

STIFFNESS = 10.0
GAP_SCALE = 0.05


def spread(block, axis, source):
    block = jnp.where(lax.axis_index(axis) == source, block, jnp.zeros_like(block))
    return lax.psum(block, axis)


def with_halo(cells, sides, width):
    for axis, dim in sides:
        count = lax.axis_size(axis)
        ends = count - 1
        head = lax.slice_in_dim(cells, 0, width, axis=dim)
        tail = lax.slice_in_dim(cells, cells.shape[dim] - width, cells.shape[dim], axis=dim)
        cells = jnp.concatenate(
            [
                lax.ppermute(tail, axis, [(i, (i + 1) % count) for i in range(ends)]),
                cells,
                lax.ppermute(head, axis, [((i + 1) % count, i) for i in range(ends)]),
            ],
            axis=dim,
        )
    return cells


def corner_forces(corner_a, corner_b, corner_c, corner_e, zone_load, zone_live):
    first_dx = 1.0 + corner_c[0] - corner_a[0]
    first_dy = 1.0 + corner_c[1] - corner_a[1]
    second_dx = -1.0 + corner_e[0] - corner_b[0]
    second_dy = 1.0 + corner_e[1] - corner_b[1]
    zone_area = 0.5 * (first_dx * second_dy - second_dx * first_dy)
    safe_area = jnp.where(zone_live, zone_area, 1.0)
    half_press = jnp.where(zone_live, 0.2 * zone_load / safe_area, 0.0)
    force_a = jnp.stack([-half_press * second_dy, half_press * second_dx])
    force_b = jnp.stack([half_press * first_dy, -half_press * first_dx])
    return (safe_area, force_a, force_b, -force_a, -force_b)


def contact_terms(slave_disp, seg_start, seg_end, side_flags, live_mask):
    rel_x = slave_disp[0] - seg_start[0] + 0.5
    rel_y = slave_disp[1] - seg_start[1]
    along_x = 1.0 + seg_end[0] - seg_start[0]
    along_y = seg_end[1] - seg_start[1]
    along_sq = along_x * along_x + along_y * along_y
    length = jnp.sqrt(along_sq)
    fraction = (rel_x * along_x + rel_y * along_y) / along_sq
    normal_x = -along_y / length
    normal_y = along_x / length
    gap_size = normal_x * rel_x + normal_y * rel_y
    side_sign = 1.0 - 2.0 * side_flags.astype(jnp.float32)
    magnitude = jnp.where(
        live_mask, STIFFNESS * GAP_SCALE * jax.nn.softplus(-side_sign * gap_size / GAP_SCALE), 0.0
    )
    slave_push = jnp.stack([magnitude * side_sign * normal_x, magnitude * side_sign * normal_y])
    react_first = jnp.stack(
        [
            -(1.0 - fraction) * slave_push[0],
            -(1.0 - fraction) * slave_push[1],
            (1.0 - fraction) * magnitude,
        ]
    )
    react_second = jnp.stack(
        [-fraction * slave_push[0], -fraction * slave_push[1], fraction * magnitude]
    )
    return (slave_push, react_first, react_second)


def shards(
    node_disp,
    node_vel,
    node_mass,
    zone_mass,
    zone_energy,
    master_block,
    owner,
    pair_node,
    pair_segment,
    pair_side,
    pair_count,
):
    row_count = node_disp.shape[1]
    col_count = node_disp.shape[2]
    row_base = lax.axis_index("gx") * row_count
    col_base = lax.axis_index("gy") * col_count
    total_rows = row_count * lax.axis_size("gx")
    total_cols = col_count * lax.axis_size("gy")
    surface = spread(master_block[0], ("gx", "gy"), owner[0])
    packed = jnp.concatenate([node_disp, (zone_energy * zone_mass)[None]], axis=0)
    extended = with_halo(packed.astype(jnp.bfloat16), (("gx", 1), ("gy", 2)), 1).astype(
        packed.dtype
    )
    zone_rows = row_base - 1 + jnp.arange(row_count + 1, dtype=jnp.int32)
    zone_cols = col_base - 1 + jnp.arange(col_count + 1, dtype=jnp.int32)
    zone_live = (
        (zone_rows[:, None] >= 0)
        & (zone_rows[:, None] < total_rows - 1)
        & (zone_cols[None, :] >= 0)
        & (zone_cols[None, :] < total_cols - 1)
    )
    safe_area, force_a, force_b, force_c, force_e = corner_forces(
        extended[:2, : row_count + 1, : col_count + 1],
        extended[:2, 1:, : col_count + 1],
        extended[:2, 1:, 1:],
        extended[:2, : row_count + 1, 1:],
        extended[2, : row_count + 1, : col_count + 1],
        zone_live,
    )
    node_force = (
        force_a[:, 1:, 1:]
        + force_b[:, :row_count, 1:]
        + force_c[:, :row_count, :col_count]
        + force_e[:, 1:, :col_count]
    )
    own_area = safe_area[1:, 1:]
    own_live = zone_live[1:, 1:]
    zone_ratio = jnp.where(own_live, jnp.sqrt(own_area) / jnp.sqrt(0.56 * zone_energy), 1e30)
    step_size = 0.3 * lax.pmin(jnp.min(zone_ratio), ("gx", "gy"))
    coords = surface[0:2].astype(jnp.float32)
    flat_disp = node_disp.reshape(2, row_count * col_count)
    live_count = pair_count[0]
    block_count = (live_count + 127) // 128
    surface_nodes = surface.shape[1]

    def contact_block(block_index, loop_state):
        pushed, reaction = loop_state
        first_pair = block_index * 128
        slave_nodes = lax.dynamic_slice_in_dim(pair_node[0], first_pair, 128)
        segment_ids = lax.dynamic_slice_in_dim(pair_segment[0], first_pair, 128)
        side_flags = lax.dynamic_slice_in_dim(pair_side[0], first_pair, 128)
        live_mask = first_pair + jnp.arange(128, dtype=jnp.int32) < live_count
        slave_disp = jnp.take(flat_disp, slave_nodes, axis=1)
        seg_start = jnp.take(coords, segment_ids, axis=1)
        seg_end = jnp.take(coords, segment_ids + 1, axis=1)
        slave_push, react_first, react_second = contact_terms(
            slave_disp, seg_start, seg_end, side_flags, live_mask
        )
        pushed = pushed.at[:, slave_nodes].add(slave_push)
        reaction = (
            reaction.at[:, segment_ids].add(react_first).at[:, segment_ids + 1].add(react_second)
        )
        return (pushed, reaction)

    pushed, reaction = lax.fori_loop(
        0,
        block_count,
        contact_block,
        (
            jnp.zeros((2, row_count * col_count), jnp.float32),
            jnp.zeros((3, surface_nodes), jnp.float32),
        ),
    )
    total_force = node_force + pushed.reshape(2, row_count, col_count)
    new_vel = node_vel + step_size * total_force / node_mass
    new_disp = node_disp + step_size * new_vel
    share_width = surface_nodes // (lax.axis_size("gx") * lax.axis_size("gy"))
    my_index = lax.axis_index("gx") * lax.axis_size("gy") + lax.axis_index("gy")
    summed = lax.psum(reaction, ("gx", "gy"))
    reaction_share = lax.dynamic_slice_in_dim(summed, my_index * share_width, share_width, 1)
    prior_impulse = lax.dynamic_slice_in_dim(
        surface[2:4], my_index * share_width, share_width, 1
    ).astype(jnp.float32)
    master_impulse = jnp.concatenate(
        [prior_impulse + step_size * reaction_share[0:2], step_size * reaction_share[2:3]], axis=0
    )
    return (new_vel, new_disp, master_impulse)


def solution(mesh):
    in_specs = (
        P(None, "gx", "gy"),
        P(None, "gx", "gy"),
        P("gx", "gy"),
        P("gx", "gy"),
        P("gx", "gy"),
        P(("gx", "gy"), None, None),
        P(),
        P(("gx", "gy"), None),
        P(("gx", "gy"), None),
        P(("gx", "gy"), None),
        P(("gx", "gy")),
    )
    out_specs = (P(None, "gx", "gy"), P(None, "gx", "gy"), P(None, ("gx", "gy")))
    return jax.shard_map(shards, mesh=mesh, in_specs=in_specs, out_specs=out_specs, check_vma=False)
```

profile of v0, /device:TPU:0, one launch (start us, length us, event | category | flops | bytes accessed | tf_op | source)
XLA Modules:
  0.0 288.3 jit_solution(1729171996044898759)
XLA Ops:
  0.6 0.9 convert.7
  1.5 0.8 fusion.25
  2.3 2.4 collective-permute-start
  4.7 1.3 collective-permute-start.1
  6.6 3.4 %copy.43 = f32[2,32,256]{0,2,1:T(8,128)} copy(f32[2,32,256]{2,1,0:T(8,128)} %param.15) | data formatting | bytes 131072 | tf_op args[0]
  10.7 44.0 %psum.14 = bf16[4,1024]{1,0:T(4,128)(2,1)S(1)} all-reduce(bf16[4,1024]{1,0:T(4,128)(2,1)S(1)} %select_bitcast_fusion.3), channel_id=1, replica_groups=mesh['gx'=8,'gy'=4] {'gx','gy'}, use_global_device_ids=true, to_apply=%region_2.3 | all-reduce | flops 4096 | bytes 16384 | tf_op jit(solution)/shard_map/psum | solution.py:12
  54.7 0.2 copy.44
  54.9 2.2 broadcast_in_dim.60
  57.2 51.2 %while.14 = (s32[]{:T(128)}, f32[2,8192]{0,1:T(8,128)}, f32[3,1024]{0,1:T(8,128)S(1)}, s32[]{:T(128)}, s32[1,1024]{1,0:T(1,128)}, /*index=5*/s32[]{:T(128)}, s32...) while((s32[]{:T(128)}, f32[2,8192]{0,1:T(8,128)}, ...), condition=%wide.region_7.9_spmd, body=%wide.region_3.8_spmd.sunk | while | flops 17542 | bytes 83919 | solution.py:149
  57.2 0.7 fusion.36
  57.9 0.7 fusion.37
  58.6 2.8 gather_fusion.2
  61.5 0.7 compare_and_fusion.5
  62.2 0.6 gather_fusion
  62.9 0.6 gather_fusion.1
  63.6 1.4 negate_multiply_fusion.9
  65.0 0.7 negate_multiply_fusion.10
  65.7 0.1 copy.57
  65.8 5.3 %scatter_fusion = f32[2,8192]{0,1:T(8,128)} fusion(f32[2,8192]{0,1:T(8,128)} %get-tuple-element.335, s32[128]{0:T(128)S(1)} %get-tuple-element.302, f32[128,2]{1,0:T(8,128)S(1)} %copy.57), kind=kCustom, calls=%fused_computation.3.clone.1 | custom fusion | flops 256 | bytes 3584 | tf_op jit(solution)/shard_map/while/body/scatter-add | solution.py:143
  71.1 0.1 copy.58
  71.2 1.5 scatter_fusion.1
  72.7 0.1 copy.59
  72.8 1.5 scatter_fusion.2
  74.3 0.7 fusion.36
  75.0 0.7 fusion.37
  75.6 2.8 gather_fusion.2
  78.5 0.7 compare_and_fusion.5
  79.2 0.6 gather_fusion
  80.0 0.6 gather_fusion.1
  80.7 1.4 negate_multiply_fusion.9
  82.1 0.7 negate_multiply_fusion.10
  82.8 0.1 copy.57
  82.9 5.3 %scatter_fusion = f32[2,8192]{0,1:T(8,128)} fusion(f32[2,8192]{0,1:T(8,128)} %get-tuple-element.335, s32[128]{0:T(128)S(1)} %get-tuple-element.302, f32[128,2]{1,0:T(8,128)S(1)} %copy.57), kind=kCustom, calls=%fused_computation.3.clone.1 | custom fusion | flops 256 | bytes 3584 | tf_op jit(solution)/shard_map/while/body/scatter-add | solution.py:143
  88.2 0.1 copy.58
  88.3 1.5 scatter_fusion.1
  89.8 0.1 copy.59
  89.9 1.5 scatter_fusion.2
  91.4 0.7 fusion.36
  92.0 0.7 fusion.37
  92.7 2.8 gather_fusion.2
  95.6 0.7 compare_and_fusion.5
  96.3 0.6 gather_fusion
  97.1 0.6 gather_fusion.1
  97.8 1.4 negate_multiply_fusion.9
  99.1 0.7 negate_multiply_fusion.10
  99.8 0.1 copy.57
  99.9 5.3 %scatter_fusion = f32[2,8192]{0,1:T(8,128)} fusion(f32[2,8192]{0,1:T(8,128)} %get-tuple-element.335, s32[128]{0:T(128)S(1)} %get-tuple-element.302, f32[128,2]{1,0:T(8,128)S(1)} %copy.57), kind=kCustom, calls=%fused_computation.3.clone.1 | custom fusion | flops 256 | bytes 3584 | tf_op jit(solution)/shard_map/while/body/scatter-add | solution.py:143
  105.2 0.1 copy.58
  105.4 1.5 scatter_fusion.1
  107.0 1.5 scatter_fusion.2
  108.5 0.2 copy.46
  108.8 121.9 %psum.15 = f32[3,1024]{1,0:T(4,128)S(1)} all-reduce(f32[3,1024]{1,0:T(4,128)S(1)} %copy.46), channel_id=1, replica_groups=mesh['gx'=8,'gy'=4] {'gx','gy'}, use_global_device_ids=true, to_apply=%region_8.10 | all-reduce | flops 3072 | bytes 24576 | tf_op jit(solution)/shard_map/psum | solution.py:163
  230.8 4.8 %collective-permute-start.2 = (bf16[3,34,1]{2,1,0:T(8,128)(2,1)S(1)}, bf16[3,34,1]{2,1,0:T(8,128)(2,1)S(1)}, u32[]{:S(2)}, u32[]{:S(2)}) collective-permute-start(bf16[3,34,1]{2,1,0:T(8,128)(2,1)S(1)} %get-tuple-element.212), channel_id=1, source_target_pairs={{0,1},{1,2},{2,3},{4,5},{5,6},{6,7},{8,9},{9,10},{10,11},{12,13},{... | collective-permute-start | bytes 620 | tf_op jit(solution)/shard_map/ppermute | solution.py:23
  235.6 1.3 collective-permute-start.3
  237.0 0.2 collective-permute-done.2
  237.1 4.2 %collective-permute-done.3 = bf16[3,34,1]{2,1,0:T(8,128)(2,1)S(1)} collective-permute-done((bf16[3,34,1]{2,1,0:T(8,128)(2,1)S(1)}, bf16[3,34,1]{2,1,0:T(8,128)(2,1)S(1)}, u32[]{:S(2)}, u32[]{:S(2)}) %collective-permute-start.3) | collective-permute-done | bytes 236 | tf_op jit(solution)/shard_map/ppermute | solution.py:25
  241.4 0.1 maximum_convert_fusion
  241.5 0.1 fusion.26
  241.7 0.7 fusion.24
  242.4 2.8 copy.47
  245.2 40.9 %pmin.7 = f32[]{:T(128)} all-reduce(f32[]{:T(128)} %fusion.24), channel_id=1, replica_groups=mesh['gx'=8,'gy'=4] {'gx','gy'}, use_global_device_ids=true, to_apply=%region_1.2 | all-reduce | flops 1 | bytes 8 | tf_op jit(solution)/shard_map/pmin | solution.py:123
  286.8 0.1 negate_multiply_fusion.5
  286.9 0.6 pad_maximum_fusion.5
  287.5 0.8 multiply_add_fusion.1
  (67 shorter events, 1.4 us)
Async XLA Ops:
  0.6 10.0 %copy-start.4 = (bf16[1,4,1024]{2,1,0:T(4,128)(2,1)S(1)}, bf16[1,4,1024]{2,1,0:T(4,128)(2,1)}, u32[]{:S(2)}) copy-start(bf16[1,4,1024]{2,1,0:T(4,128)(2,1)} %param.20) | copy-start | bytes 24580
  2.3 228.4 %collective-permute-start = (bf16[3,1,256]{2,1,0:T(2,128)(2,1)S(1)}, bf16[3,1,256]{2,1,0:T(2,128)(2,1)S(1)}, u32[]{:S(2)}, u32[]{:S(2)}) collective-permute-start(bf16[3,1,256]{2,1,0:T(2,128)(2,1)S(1)} %get-tuple-element.214), channel_id=1, source_target_pairs={{0,4},{4,8},{8,12},{12,16},{16,20},{20,24},{24,28},{1,5},{5,9},{9,... | collective-permute-start | bytes 4616 | tf_op jit(solution)/shard_map/ppermute | solution.py:23
  4.7 226.0 %collective-permute-start.1 = (bf16[3,1,256]{2,1,0:T(2,128)(2,1)S(1)}, bf16[3,1,256]{2,1,0:T(2,128)(2,1)S(1)}, u32[]{:S(2)}, u32[]{:S(2)}) collective-permute-start(bf16[3,1,256]{2,1,0:T(2,128)(2,1)S(1)} %get-tuple-element.215), channel_id=1, source_target_pairs={{4,0},{8,4},{12,8},{16,12},{20,16},{24,20},{28,24},{5,1},{9,5},{13... | collective-permute-start | bytes 4616 | tf_op jit(solution)/shard_map/ppermute | solution.py:25
  54.9 186.7 %copy-start.1 = (f32[32,256]{1,0:T(8,128)S(1)}, f32[32,256]{1,0:T(8,128)}, u32[]{:S(2)}) copy-start(f32[32,256]{1,0:T(8,128)} %param.19) | copy-start | bytes 98308
  108.4 179.1 %copy-start = (f32[2,32,256]{2,1,0:T(8,128)S(1)}, f32[2,32,256]{2,1,0:T(8,128)}, u32[]{:S(2)}) copy-start(f32[2,32,256]{2,1,0:T(8,128)} %param.15) | copy-start | bytes 196612
  108.4 179.1 %copy-start.2 = (f32[2,32,256]{2,1,0:T(8,128)S(1)}, f32[2,32,256]{2,1,0:T(8,128)}, u32[]{:S(2)}) copy-start(f32[2,32,256]{2,1,0:T(8,128)} %param.16) | copy-start | bytes 196612
  108.5 179.1 %copy-start.3 = (f32[32,256]{1,0:T(8,128)S(1)}, f32[32,256]{1,0:T(8,128)}, u32[]{:S(2)}) copy-start(f32[32,256]{1,0:T(8,128)} %param.17) | copy-start | bytes 98308
  230.8 6.3 %collective-permute-start.2 = (bf16[3,34,1]{2,1,0:T(8,128)(2,1)S(1)}, bf16[3,34,1]{2,1,0:T(8,128)(2,1)S(1)}, u32[]{:S(2)}, u32[]{:S(2)}) collective-permute-start(bf16[3,34,1]{2,1,0:T(8,128)(2,1)S(1)} %get-tuple-element.212), channel_id=1, source_target_pairs={{0,1},{1,2},{2,3},{4,5},{5,6},{6,7},{8,9},{9,10},{10,11},{12,13},{... | collective-permute-start | bytes 620 | tf_op jit(solution)/shard_map/ppermute | solution.py:23
  235.6 5.8 %collective-permute-start.3 = (bf16[3,34,1]{2,1,0:T(8,128)(2,1)S(1)}, bf16[3,34,1]{2,1,0:T(8,128)(2,1)S(1)}, u32[]{:S(2)}, u32[]{:S(2)}) collective-permute-start(bf16[3,34,1]{2,1,0:T(8,128)(2,1)S(1)} %get-tuple-element.213), channel_id=1, source_target_pairs={{1,0},{2,1},{3,2},{5,4},{6,5},{7,6},{9,8},{10,9},{11,10},{13,12},{... | collective-permute-start | bytes 620 | tf_op jit(solution)/shard_map/ppermute | solution.py:25
where the time goes:
time: 290 us; the launch traced here: 288 us
  blocking collectives  207 us (71%)
  other arithmetic  41.3 us (14%)
  local copies, waits for them, and re-layouts  23 us (8%)
  starting transfers between devices  9.75 us (3%)
  waiting for transfers between devices  4.41 us (2%)
    psum x1, blocking collectives, shards(): summed = lax.psum(reaction, ('gx', 'gy'))  122 us
    psum x1, blocking collectives, spread(): return lax.psum(block, axis)  44 us
    pmin x1, blocking collectives, shards(): step_size = 0.3 * lax.pmin(jnp.min(zone_ratio), ('gx', 'gy'))  40.9 us
    scatter-add x3, other arithmetic, contact_block(): pushed = pushed.at[:, slave_nodes].add(slave_push)  15.9 us
    scatter-add x6, other arithmetic, contact_block(): reaction.at[:, segment_ids].add(react_first).at[:, segment_ids + 1]  8.71 us
    gather x6, local copies, waits for them, and re-layouts, contact_block(): slave_disp = jnp.take(flat_disp, slave_nodes, axis=1)  8.68 us
    ppermute x2, starting transfers between devices, with_halo(): lax.ppermute(tail, axis, [(i, (i + 1) % count) for i in range(ends)])  7.16 us
  transfers between devices with their start and end apart: 4, of which 2 were waited for; matrix products, arithmetic and copies ran while one was open for 20% of the time, Pallas kernels for 0%

commit v1 on v0

--- a/solution.py
+++ b/solution.py
@@ -160,7 +160,8 @@
     new_disp = node_disp + step_size * new_vel
     share_width = surface_nodes // (lax.axis_size("gx") * lax.axis_size("gy"))
     my_index = lax.axis_index("gx") * lax.axis_size("gy") + lax.axis_index("gy")
-    summed = lax.psum(reaction, ("gx", "gy"))
+    parts = lax.all_gather(reaction, ("gx", "gy"))
+    summed = jnp.sum(parts, axis=0)
     reaction_share = lax.dynamic_slice_in_dim(summed, my_index * share_width, share_width, 1)
     prior_impulse = lax.dynamic_slice_in_dim(
         surface[2:4], my_index * share_width, share_width, 1

time: 290 us -> 316 us (1.090)
  blocking collectives: 207 us -> 233 us
    all_gather x0 -> x1, blocking collectives: none -> 133 us  [shards(): parts = lax.all_gather(reaction, ('gx', 'gy'))]
    psum x1 -> x0, blocking collectives: 122 us -> none  [shards(): summed = lax.psum(reaction, ('gx', 'gy'))]
    pmin x1, blocking collectives: 40.9 us -> 55.9 us  [shards(): step_size = 0.3 * lax.pmin(jnp.min(zone_ratio), ('gx', 'gy'))]
  transfers between devices with their start and end apart: 4 -> 4, of which waited for: 2 -> 2; matrix products, arithmetic and copies ran while one was open for 20% -> 18% of each run, Pallas kernels for 0% -> 0%
where the time goes in v1:
time: 316 us; the launch traced here: 314 us
  blocking collectives  233 us (74%)
  other arithmetic  41.4 us (13%)
  local copies, waits for them, and re-layouts  23 us (7%)
  starting transfers between devices  9.17 us (3%)
  waiting for transfers between devices  4.41 us (1%)
    all_gather x1, blocking collectives, shards(): parts = lax.all_gather(reaction, ('gx', 'gy'))  133 us
    pmin x1, blocking collectives, shards(): step_size = 0.3 * lax.pmin(jnp.min(zone_ratio), ('gx', 'gy'))  55.9 us
    psum x1, blocking collectives, spread(): return lax.psum(block, axis)  44 us
    scatter-add x3, other arithmetic, contact_block(): pushed = pushed.at[:, slave_nodes].add(slave_push)  15.9 us
    scatter-add x6, other arithmetic, contact_block(): reaction.at[:, segment_ids].add(react_first).at[:, segment_ids + 1]  8.71 us
    gather x6, local copies, waits for them, and re-layouts, contact_block(): slave_disp = jnp.take(flat_disp, slave_nodes, axis=1)  8.68 us
    ppermute x2, starting transfers between devices, with_halo(): lax.ppermute(tail, axis, [(i, (i + 1) % count) for i in range(ends)])  6.59 us
  transfers between devices with their start and end apart: 4, of which 2 were waited for; matrix products, arithmetic and copies ran while one was open for 18% of the time, Pallas kernels for 0%

profile of v1, /device:TPU:0, one launch (start us, length us, event | category | flops | bytes accessed | tf_op | source)
XLA Modules:
  0.0 314.3 jit_solution(3295217070302964298)
XLA Ops:
  0.6 0.9 convert.7
  1.5 0.8 fusion.25
  2.3 2.4 collective-permute-start
  4.7 1.3 collective-permute-start.1
  6.6 3.4 %copy.65 = f32[2,32,256]{0,2,1:T(8,128)} copy(f32[2,32,256]{2,1,0:T(8,128)} %param.15) | data formatting | bytes 131072 | tf_op args[0]
  10.7 44.0 %psum.7 = bf16[4,1024]{1,0:T(4,128)(2,1)S(1)} all-reduce(bf16[4,1024]{1,0:T(4,128)(2,1)S(1)} %select_bitcast_fusion.3), channel_id=1, replica_groups=mesh['gx'=8,'gy'=4] {'gx','gy'}, use_global_device_ids=true, to_apply=%region_2.3 | all-reduce | flops 4096 | bytes 16384 | tf_op jit(solution)/shard_map/psum | solution.py:12
  54.7 0.2 copy.66
  54.9 2.2 broadcast_in_dim.60
  57.2 51.2 %while.14 = (s32[]{:T(128)}, f32[2,8192]{0,1:T(8,128)}, f32[3,1024]{0,1:T(8,128)S(1)}, s32[]{:T(128)}, s32[1,1024]{1,0:T(1,128)}, /*index=5*/s32[]{:T(128)}, s32...) while((s32[]{:T(128)}, f32[2,8192]{0,1:T(8,128)}, ...), condition=%wide.region_7.9_spmd, body=%wide.region_3.8_spmd.sunk | while | flops 17542 | bytes 83919 | solution.py:149
  57.2 0.7 fusion.36
  57.9 0.7 fusion.37
  58.6 2.8 gather_fusion.2
  61.5 0.7 compare_and_fusion.5
  62.2 0.6 gather_fusion
  62.9 0.6 gather_fusion.1
  63.6 1.4 negate_multiply_fusion.9
  65.0 0.7 negate_multiply_fusion.10
  65.7 0.1 copy.88
  65.8 5.3 %scatter_fusion = f32[2,8192]{0,1:T(8,128)} fusion(f32[2,8192]{0,1:T(8,128)} %get-tuple-element.348, s32[128]{0:T(128)S(1)} %get-tuple-element.315, f32[128,2]{1,0:T(8,128)S(1)} %copy.88), kind=kCustom, calls=%fused_computation.3.clone.1 | custom fusion | flops 256 | bytes 3584 | tf_op jit(solution)/shard_map/while/body/scatter-add | solution.py:143
  71.1 0.1 copy.89
  71.2 1.5 scatter_fusion.1
  72.7 0.1 copy.90
  72.8 1.5 scatter_fusion.2
  74.3 0.7 fusion.36
  75.0 0.7 fusion.37
  75.6 2.8 gather_fusion.2
  78.5 0.7 compare_and_fusion.5
  79.2 0.6 gather_fusion
  80.0 0.6 gather_fusion.1
  80.7 1.4 negate_multiply_fusion.9
  82.1 0.7 negate_multiply_fusion.10
  82.7 0.1 copy.88
  82.9 5.3 %scatter_fusion = f32[2,8192]{0,1:T(8,128)} fusion(f32[2,8192]{0,1:T(8,128)} %get-tuple-element.348, s32[128]{0:T(128)S(1)} %get-tuple-element.315, f32[128,2]{1,0:T(8,128)S(1)} %copy.88), kind=kCustom, calls=%fused_computation.3.clone.1 | custom fusion | flops 256 | bytes 3584 | tf_op jit(solution)/shard_map/while/body/scatter-add | solution.py:143
  88.2 0.1 copy.89
  88.3 1.5 scatter_fusion.1
  89.8 0.1 copy.90
  89.9 1.5 scatter_fusion.2
  91.4 0.7 fusion.36
  92.0 0.7 fusion.37
  92.7 2.8 gather_fusion.2
  95.6 0.7 compare_and_fusion.5
  96.3 0.6 gather_fusion
  97.0 0.6 gather_fusion.1
  97.8 1.4 negate_multiply_fusion.9
  99.1 0.7 negate_multiply_fusion.10
  99.8 0.1 copy.88
  99.9 5.3 %scatter_fusion = f32[2,8192]{0,1:T(8,128)} fusion(f32[2,8192]{0,1:T(8,128)} %get-tuple-element.348, s32[128]{0:T(128)S(1)} %get-tuple-element.315, f32[128,2]{1,0:T(8,128)S(1)} %copy.88), kind=kCustom, calls=%fused_computation.3.clone.1 | custom fusion | flops 256 | bytes 3584 | tf_op jit(solution)/shard_map/while/body/scatter-add | solution.py:143
  105.2 0.1 copy.89
  105.4 1.5 scatter_fusion.1
  106.9 1.5 scatter_fusion.2
  108.5 0.2 copy.68
  108.8 133.4 %all-gather.1 = f32[32,3,1024]{2,1,0:T(4,128)S(1)} all-gather(f32[1,3,1024]{2,1,0:T(4,128)S(1)} %bitcast.76), channel_id=2, replica_groups=mesh['gx'=8,'gy'=4] {'gx','gy'}, dimensions={0}, use_global_device_ids=true | all-gather | bytes 405504 | tf_op jit(solution)/shard_map/all_gather | solution.py:163
  242.4 4.2 %collective-permute-start.2 = (bf16[3,34,1]{2,1,0:T(8,128)(2,1)S(1)}, bf16[3,34,1]{2,1,0:T(8,128)(2,1)S(1)}, u32[]{:S(2)}, u32[]{:S(2)}) collective-permute-start(bf16[3,34,1]{2,1,0:T(8,128)(2,1)S(1)} %get-tuple-element.225), channel_id=1, source_target_pairs={{0,1},{1,2},{2,3},{4,5},{5,6},{6,7},{8,9},{9,10},{10,11},{12,13},{... | collective-permute-start | bytes 620 | tf_op jit(solution)/shard_map/ppermute | solution.py:23
  246.6 1.3 collective-permute-start.3
  248.0 0.2 collective-permute-done.2
  248.2 4.2 %collective-permute-done.3 = bf16[3,34,1]{2,1,0:T(8,128)(2,1)S(1)} collective-permute-done((bf16[3,34,1]{2,1,0:T(8,128)(2,1)S(1)}, bf16[3,34,1]{2,1,0:T(8,128)(2,1)S(1)}, u32[]{:S(2)}, u32[]{:S(2)}) %collective-permute-start.3) | collective-permute-done | bytes 236 | tf_op jit(solution)/shard_map/ppermute | solution.py:25
  252.4 0.1 maximum_convert_fusion
  252.5 0.1 fusion.26
  252.7 0.7 fusion.24
  253.4 2.8 copy.71
  256.2 55.9 %pmin.7 = f32[]{:T(128)} all-reduce(f32[]{:T(128)} %fusion.24), channel_id=1, replica_groups=mesh['gx'=8,'gy'=4] {'gx','gy'}, use_global_device_ids=true, to_apply=%region_1.2 | all-reduce | flops 1 | bytes 8 | tf_op jit(solution)/shard_map/pmin | solution.py:123
  312.8 0.1 negate_multiply_fusion.5
  313.0 0.6 pad_maximum_fusion.5
  313.6 0.8 multiply_add_fusion.1
  (68 shorter events, 1.5 us)
Async XLA Ops:
  0.6 10.0 %copy-start.4 = (bf16[1,4,1024]{2,1,0:T(4,128)(2,1)S(1)}, bf16[1,4,1024]{2,1,0:T(4,128)(2,1)}, u32[]{:S(2)}) copy-start(bf16[1,4,1024]{2,1,0:T(4,128)(2,1)} %param.20) | copy-start | bytes 24580
  2.3 240.0 %collective-permute-start = (bf16[3,1,256]{2,1,0:T(2,128)(2,1)S(1)}, bf16[3,1,256]{2,1,0:T(2,128)(2,1)S(1)}, u32[]{:S(2)}, u32[]{:S(2)}) collective-permute-start(bf16[3,1,256]{2,1,0:T(2,128)(2,1)S(1)} %get-tuple-element.227), channel_id=1, source_target_pairs={{0,4},{4,8},{8,12},{12,16},{16,20},{20,24},{24,28},{1,5},{5,9},{9,... | collective-permute-start | bytes 4616 | tf_op jit(solution)/shard_map/ppermute | solution.py:23
  4.7 237.6 %collective-permute-start.1 = (bf16[3,1,256]{2,1,0:T(2,128)(2,1)S(1)}, bf16[3,1,256]{2,1,0:T(2,128)(2,1)S(1)}, u32[]{:S(2)}, u32[]{:S(2)}) collective-permute-start(bf16[3,1,256]{2,1,0:T(2,128)(2,1)S(1)} %get-tuple-element.228), channel_id=1, source_target_pairs={{4,0},{8,4},{12,8},{16,12},{20,16},{24,20},{28,24},{5,1},{9,5},{13... | collective-permute-start | bytes 4616 | tf_op jit(solution)/shard_map/ppermute | solution.py:25
  57.2 195.5 %copy-start.1 = (f32[32,256]{1,0:T(8,128)S(1)}, f32[32,256]{1,0:T(8,128)}, u32[]{:S(2)}) copy-start(f32[32,256]{1,0:T(8,128)} %param.19) | copy-start | bytes 98308
  108.4 205.1 %copy-start = (f32[2,32,256]{2,1,0:T(8,128)S(1)}, f32[2,32,256]{2,1,0:T(8,128)}, u32[]{:S(2)}) copy-start(f32[2,32,256]{2,1,0:T(8,128)} %param.15) | copy-start | bytes 196612
  108.4 205.1 %copy-start.2 = (f32[2,32,256]{2,1,0:T(8,128)S(1)}, f32[2,32,256]{2,1,0:T(8,128)}, u32[]{:S(2)}) copy-start(f32[2,32,256]{2,1,0:T(8,128)} %param.16) | copy-start | bytes 196612
  108.4 205.1 %copy-start.3 = (f32[32,256]{1,0:T(8,128)S(1)}, f32[32,256]{1,0:T(8,128)}, u32[]{:S(2)}) copy-start(f32[32,256]{1,0:T(8,128)} %param.17) | copy-start | bytes 98308
  242.4 5.8 %collective-permute-start.2 = (bf16[3,34,1]{2,1,0:T(8,128)(2,1)S(1)}, bf16[3,34,1]{2,1,0:T(8,128)(2,1)S(1)}, u32[]{:S(2)}, u32[]{:S(2)}) collective-permute-start(bf16[3,34,1]{2,1,0:T(8,128)(2,1)S(1)} %get-tuple-element.225), channel_id=1, source_target_pairs={{0,1},{1,2},{2,3},{4,5},{5,6},{6,7},{8,9},{9,10},{10,11},{12,13},{... | collective-permute-start | bytes 620 | tf_op jit(solution)/shard_map/ppermute | solution.py:23
  246.6 5.8 %collective-permute-start.3 = (bf16[3,34,1]{2,1,0:T(8,128)(2,1)S(1)}, bf16[3,34,1]{2,1,0:T(8,128)(2,1)S(1)}, u32[]{:S(2)}, u32[]{:S(2)}) collective-permute-start(bf16[3,34,1]{2,1,0:T(8,128)(2,1)S(1)} %get-tuple-element.226), channel_id=1, source_target_pairs={{1,0},{2,1},{3,2},{5,4},{6,5},{7,6},{9,8},{10,9},{11,10},{13,12},{... | collective-permute-start | bytes 620 | tf_op jit(solution)/shard_map/ppermute | solution.py:25
